TPU v7x, 32 devices: a whole 2x2x4 slice. The times are simulated.
32 devices in a mesh: group: 4 (over y, x), depth: 2 (over core), mp: 4 (over z).
Axes of the slice: x: 2, y: 2, z: 4, core: 2. Of those that a mesh axis runs over, the one named last changes fastest.
Arguments:
- states: bfloat16 [64, 4096], P(('group', 'depth', 'mp')), may hold values from -6 to 6
- queries: bfloat16 [64, 32, 128], P('group', 'mp'), may hold values from -6 to 6
- new_keys: bfloat16 [64, 8, 128], P('group', 'mp'), may hold values from -18 to 18
- new_values: bfloat16 [64, 8, 128], P('group', 'mp'), may hold values from -24 to 24
- text_keys: bfloat16 [64, 8, 512, 128], P('group', 'mp', 'depth'), may hold values from -6 to 6
- text_values: bfloat16 [64, 8, 512, 128], P('group', 'mp', 'depth'), may hold values from -24 to 24
- text_length: int32 [64], P('group'), may hold values from 2 to 512
- image_keys: bfloat16 [32, 8, 576, 128], P('group', 'mp'), may hold values from -6 to 6
- image_values: bfloat16 [32, 8, 576, 128], P('group', 'mp'), may hold values from -24 to 24
- image_slot: int32 [32], replicated, may hold values from 0 to 31, as said below
- block_list: int32 [4, 32], replicated, may hold values from 0 to 31, as said below
- block_count: int32 [4], replicated, may hold values from 16 to 32, as said below
- image_first: int32 [64], P('group'), may hold values from 0 to 31, as said below
- image_count: int32 [64], P('group'), may hold values from 1 to 2
- out_weight: bfloat16 [4096, 4096], P('mp'), may hold values from -0.09375 to 0.09375
- norm_gain: float32 [4096], replicated, may hold values from 0.5 to 1.5
- gate_weight: bfloat16 [4096, 14336], P(None, ('group', 'mp')), may hold values from -0.09375 to 0.09375
- up_weight: bfloat16 [4096, 14336], P(None, ('group', 'mp')), may hold values from -0.09375 to 0.09375
- down_weight: bfloat16 [14336, 4096], P(('group', 'mp')), may hold values from -0.046875 to 0.046875
Outputs:
- attention: bfloat16 [64, 32, 128], P(('group', 'depth'), 'mp')
- layer_out: bfloat16 [64, 4096], P(('group', 'depth', 'mp'))
Inputs may be any that keep to these rules, and one draw needn't show every extreme that they name: `image_slot`: a permutation. The owner group of hash k is image_slot[k] // 8. `block_list`: the hashes of one group's list are distinct. Among one group's places with the same remainder modulo 2, at most 4 belongs to any one owner group; some group has block_count 32, and there every owner group holds exactly 4 place of every remainder. `block_count`: the sum of image_count over the group's requests. The requests of a group take consecutive list places in request order: image_first is the sum of image_count over the group's earlier requests.
All inputs are finite; a program needn't handle non-finite values.
Results may differ from a plain program's by a relative error of at most 0.012.
Values may be sent and summed in bfloat16 or wider, within the bound.
A program may use at most 128 MiB of HBM per device.

v0:
```python
import math
import jax
import jax.numpy as jnp
from jax import lax
from jax.sharding import PartitionSpec as P

LOG_TWO = math.log(2.0)
MASKED_SCORE = -1e30
NORM_EPSILON = 1e-05


def merged(part, axis, combine):
    gathered = jax.tree.map(lambda a: lax.all_gather(a, axis), part)

    def take(source):
        return jax.tree.map(lambda a: lax.dynamic_index_in_dim(a, source, 0, False), gathered)

    return lax.fori_loop(
        1, lax.axis_size(axis), lambda source, state: combine(state, take(source)), take(0)
    )


def combine(first_part, second_part):
    highest = jnp.maximum(first_part[0], second_part[0])
    first_factor = jnp.exp2(first_part[0] - highest)
    second_factor = jnp.exp2(second_part[0] - highest)
    totals = first_part[1] * first_factor + second_part[1] * second_factor
    weighted = first_part[2] * first_factor[..., None] + second_part[2] * second_factor[..., None]
    return (highest, totals, weighted)


def on_device(
    states,
    queries,
    new_keys,
    new_values,
    text_keys,
    text_values,
    text_length,
    image_keys,
    image_values,
    image_slot,
    block_list,
    block_count,
    image_first,
    image_count,
    out_weight,
    norm_gain,
    gate_weight,
    up_weight,
    down_weight,
):
    groups = lax.axis_size("group")
    depths = lax.axis_size("depth")
    group_index = lax.axis_index("group")
    depth_index = lax.axis_index("depth")
    requests, head_count, head_width = queries.shape
    kv_heads = text_keys.shape[1]
    text_span = text_keys.shape[2]
    stored = image_keys.shape[0]
    listed = block_list.shape[1]
    copies = listed // (depths * groups)
    group_share = head_count // kv_heads
    scaling = 1.0 / math.sqrt(head_width)
    grouped = queries.reshape(requests, kv_heads, group_share, head_width)
    text_scores = (
        jnp.einsum("rhgd,rhpd->rhgp", grouped, text_keys, preferred_element_type=jnp.float32)
        * scaling
    )
    new_scores = (
        jnp.einsum("rhgd,rhd->rhg", grouped, new_keys, preferred_element_type=jnp.float32) * scaling
    )
    positions = depth_index * text_span + jnp.arange(text_span, dtype=jnp.int32)
    text_allowed = (positions[None, :] < text_length[:, None])[:, None, None, :]
    new_allowed = depth_index == 0
    highest = jnp.maximum(
        jnp.max(jnp.where(text_allowed, text_scores, MASKED_SCORE), axis=-1),
        jnp.where(new_allowed, new_scores, MASKED_SCORE),
    )
    levels = jnp.floor(highest / LOG_TWO)
    text_weights = jnp.where(
        text_allowed, jnp.exp(text_scores - LOG_TWO * levels[..., None]), 0.0
    ).astype(jnp.bfloat16)
    new_weights = (
        jnp.where(new_allowed, jnp.exp(new_scores - LOG_TWO * levels), 0.0)
        .astype(jnp.bfloat16)
        .astype(jnp.float32)
    )
    totals = jnp.sum(text_weights, axis=-1, dtype=jnp.float32) + new_weights
    weighted = jnp.einsum(
        "rhgp,rhpd->rhgd", text_weights, text_values, preferred_element_type=jnp.float32
    )
    weighted = weighted + new_weights[..., None] * new_values.astype(jnp.float32)[:, :, None, :]
    local_part = (levels, totals, weighted)

    def owner_table(list_row, list_count, depth):
        indices = jnp.arange(groups * copies, dtype=jnp.int32)
        places = indices * depths + depth
        hashes = jnp.take(list_row, places, axis=0)
        slot_rows = jnp.take(image_slot, hashes, axis=0)
        owners = slot_rows // stored
        within = slot_rows % stored
        active = places < list_count
        member = (
            (owners[:, None] == jnp.arange(groups, dtype=jnp.int32)[None, :]) & active[:, None]
        ).astype(jnp.int32)
        earlier = jnp.cumsum(member, axis=0) - member
        ranked = jnp.sum(earlier * member, axis=1)
        picked = member[:, :, None] * (
            ranked[:, None, None] == jnp.arange(copies, dtype=jnp.int32)[None, None, :]
        ).astype(jnp.int32)
        chosen = jnp.sum(picked * within[:, None, None], axis=0)
        placed = jnp.sum(picked * places[:, None, None], axis=0)
        present = jnp.sum(picked, axis=0) > 0
        return (chosen, placed, present)

    own_row = lax.dynamic_index_in_dim(block_list, group_index, 0, keepdims=False)
    own_count = lax.dynamic_index_in_dim(block_count, group_index, 0, keepdims=False)
    own_chosen, own_placed, own_present = owner_table(own_row, own_count, depth_index)
    finish = image_first + image_count
    in_use = (
        own_present[None]
        & (own_placed[None] >= image_first[:, None, None])
        & (own_placed[None] < finish[:, None, None])
    )
    in_use_int = in_use.astype(jnp.int32)
    every_chosen, every_placed, every_present = jax.vmap(
        lambda list_row, list_count: owner_table(list_row, list_count, depth_index)
    )(block_list, block_count)
    serve_slots = lax.dynamic_index_in_dim(every_chosen, group_index, 1, keepdims=False)
    serve_present = lax.dynamic_index_in_dim(every_present, group_index, 1, keepdims=False)
    request_numbers = jnp.arange(requests, dtype=jnp.int32)[:, None, None]
    reader = jnp.sum(in_use_int * request_numbers, axis=0)
    routed = jnp.take(queries, reader.reshape(-1), axis=0).reshape(
        groups, copies, head_count, head_width
    )
    arrived = lax.all_to_all(routed, "group", split_axis=0, concat_axis=0, tiled=True)
    arrived = arrived.reshape(groups, copies, kv_heads, group_share, head_width)
    owned_keys = jnp.take(image_keys, serve_slots, axis=0)
    owned_values = jnp.take(image_values, serve_slots, axis=0)
    owned_scores = (
        jnp.einsum("schgd,schpd->schgp", arrived, owned_keys, preferred_element_type=jnp.float32)
        * scaling
    )
    owned_allowed = serve_present[:, :, None, None, None]
    owned_high = jnp.max(jnp.where(owned_allowed, owned_scores, MASKED_SCORE), axis=-1)
    owned_levels = jnp.floor(owned_high / LOG_TWO)
    owned_weights = jnp.where(
        owned_allowed, jnp.exp(owned_scores - LOG_TWO * owned_levels[..., None]), 0.0
    ).astype(jnp.bfloat16)
    owned_totals = jnp.sum(owned_weights, axis=-1, dtype=jnp.float32)
    owned_weighted = jnp.einsum(
        "schgp,schpd->schgd", owned_weights, owned_values, preferred_element_type=jnp.float32
    )
    back_levels, back_totals, back_weighted = (
        lax.all_to_all(owned_levels, "group", split_axis=0, concat_axis=0, tiled=True),
        lax.all_to_all(owned_totals, "group", split_axis=0, concat_axis=0, tiled=True),
        lax.all_to_all(owned_weighted, "group", split_axis=0, concat_axis=0, tiled=True),
    )
    use_float = in_use.astype(jnp.float32)
    image_levels = jnp.max(
        jnp.where(in_use[:, :, :, None, None], back_levels[None], MASKED_SCORE), axis=(1, 2)
    )
    image_totals = jnp.einsum(
        "roc,ochg->rhg", use_float, back_totals, precision=lax.Precision.HIGHEST
    )
    image_weighted = jnp.einsum(
        "roc,ochgd->rhgd", use_float, back_weighted, precision=lax.Precision.HIGHEST
    )
    image_part = (image_levels, image_totals, image_weighted)
    partial_value = combine(local_part, image_part)
    merged_levels, merged_totals, merged_weighted = merged(partial_value, "depth", combine)
    attention_all = (
        (merged_weighted / merged_totals[..., None])
        .reshape(requests, head_count, head_width)
        .astype(jnp.bfloat16)
    )
    per_depth = requests // depths
    attention_half = lax.dynamic_slice_in_dim(attention_all, depth_index * per_depth, per_depth, 0)
    flattened = attention_half.reshape(per_depth, head_count * head_width)
    picked_rows = flattened
    projected = lax.psum_scatter(
        jnp.dot(picked_rows, out_weight, preferred_element_type=jnp.float32),
        "mp",
        scatter_dimension=0,
        tiled=True,
    )
    residual = states.astype(jnp.float32) + projected
    spread = jnp.mean(residual * residual, axis=-1, keepdims=True)
    normed = (residual * lax.rsqrt(spread + NORM_EPSILON) * norm_gain).astype(jnp.bfloat16)
    piece = lax.all_gather(normed, ("group", "mp"), axis=0, tiled=True)
    gate_term = jnp.dot(piece, gate_weight, preferred_element_type=jnp.float32)
    up_term = jnp.dot(piece, up_weight, preferred_element_type=jnp.float32)
    hidden = (jax.nn.silu(gate_term) * up_term).astype(jnp.bfloat16)
    picked_rows = hidden
    summed = lax.psum_scatter(
        jnp.dot(picked_rows, down_weight, preferred_element_type=jnp.float32),
        ("group", "mp"),
        scatter_dimension=0,
        tiled=True,
    )
    return (attention_half, (residual + summed).astype(jnp.bfloat16))


def solution(mesh):
    placed = (
        P(("group", "depth", "mp"), None),
        P("group", "mp", None),
        P("group", "mp", None),
        P("group", "mp", None),
        P("group", "mp", "depth", None),
        P("group", "mp", "depth", None),
        P("group"),
        P("group", "mp", None, None),
        P("group", "mp", None, None),
        P(),
        P(),
        P(),
        P("group"),
        P("group"),
        P("mp", None),
        P(),
        P(None, ("group", "mp")),
        P(None, ("group", "mp")),
        P(("group", "mp"), None),
    )
    return jax.shard_map(
        on_device,
        mesh=mesh,
        in_specs=placed,
        out_specs=(P(("group", "depth"), "mp", None), P(("group", "depth", "mp"), None)),
        check_vma=False,
    )
```

profile of v0, /device:TPU:0, one launch (start us, length us, event | category | flops | bytes accessed | tf_op | source)
XLA Modules:
  0.0 287.0 jit_solution(1384392448140040377)
XLA Ops:
  7.2 0.8 fusion.52
  8.1 0.7 gather_fusion.3
  8.8 1.3 gather_fusion.4
  10.1 1.2 dynamic_slice.43
  11.4 0.7 broadcast_compare_fusion.3
  12.4 0.2 multiply_reduce_fusion.2
  12.8 0.7 add.205
  13.5 0.9 select_reduce_fusion.4
  14.6 1.3 gather_fusion.2
  15.9 0.7 broadcast_select_fusion
  16.6 5.2 %all-to-all-start = ((bf16[4,4,8,128]{3,2,1,0:T(8,128)(2,1)}), bf16[4,4,8,128]{3,2,1,0:T(8,128)(2,1)S(1)}, u32[]{:S(2)}, u32[]{:S(2)}) async-start(bf16[4,4,8,128]{3,2,1,0:T(8,128)(2,1)} %broadcast_select_fusion), calls=%async_computation | async-start | bytes 65536 | tf_op jit(solution)/shard_map/all_to_all | solution.py:137
  21.8 0.8 copy.120
  22.6 0.7 broadcast_compare_fusion.1
  23.3 0.6 gather_fusion
  24.1 1.4 gather_fusion.1
  26.1 0.2 select_reduce_fusion.3
  26.4 0.6 multiply_reduce_fusion
  27.2 0.7 broadcast_compare_fusion
  27.9 2.3 select_reduce_fusion.1
  30.8 0.2 convert_reduce_fusion.1
  31.1 3.3 %gather_fusion.5 = bf16[16,2,576,128]{3,2,1,0:T(8,128)(2,1)} fusion(bf16[8,2,576,128]{3,2,1,0:T(8,128)(2,1)S(1)} %copy-done, s32[1024]{0:T(1024)S(1)} %pad_clamp_fusion), kind=kCustom, calls=%fused_computation.1.clone | custom fusion | bytes 9437248 | tf_op jit(solution)/shard_map/jit(_take)/gather | solution.py:139
  34.5 5.0 %gather_fusion.6 = bf16[16,2,576,128]{3,2,1,0:T(8,128)(2,1)} fusion(bf16[8,2,576,128]{3,2,1,0:T(8,128)(2,1)} %param.31, s32[1024]{0:T(1024)S(1)} %pad_clamp_fusion), kind=kCustom, calls=%fused_computation.3.clone | custom fusion | bytes 9437248 | tf_op jit(solution)/shard_map/jit(_take)/gather | solution.py:140
  39.4 4.0 %select_reduce_fusion = (f32[4,4,2,4]{3,2,1,0:T(2,128)S(1)}, f32[4,4,2,4,576]{4,3,2,1,0:T(4,128)S(1)}) fusion(pred[4,4]{1,0:T(4,128)(4,1)S(1)} %bitcast.98, bf16[4,4,2,4,128]{4,3,2,1,0:T(4,128)(2,1)S(1)} %bitcast.91, bf16[4,4,2,576,128]{4,3,2,1,0:T(8,128)(2,1)} %bitcast.83, pred[4,4]{1,0:T(4,128)(4,1)S(1)} %compare_and_fusion.1), kind=kOutput, calls=%fused_computation.29 | convolution fusion | flops 21454720 | bytes 5046816 | tf_op jit(solution)/shard_map/schgd,schpd->schgp/dot_general | solution.py:142
  43.4 0.6 multiply_floor_fusion
  44.0 4.2 %all-to-all-start.1 = ((f32[4,4,2,4]{3,2,1,0:T(2,128)}), f32[4,4,2,4]{3,2,1,0:T(2,128)S(1)}, u32[]{:S(2)}, u32[]{:S(2)}) async-start(f32[4,4,2,4]{3,2,1,0:T(2,128)} %get-tuple-element.49), calls=%async_computation.1 | async-start | bytes 32768 | tf_op jit(solution)/shard_map/all_to_all | solution.py:156
  48.2 3.2 %fusion = f32[4,4,2,4,128]{4,3,2,1,0:T(4,128)S(1)} fusion(bf16[4,4,2,576,128]{4,3,2,1,0:T(8,128)(2,1)} %bitcast.82, pred[4,4]{1,0:T(4,128)(4,1)S(1)} %compare_and_fusion.1, f32[4,4,2,4,576]{4,3,2,1,0:T(4,128)S(1)} %get-tuple-element.53, f32[4,4,2,4]{3,2,1,0:T(2,128)S(1)} %get-tuple-element.50, pred[4,4]{1,0:T(4,128)(4,1)S(1)} %bitcast.99), kind=kOutput, calls=%fused_computation.7 | convolution fusion | flops 21454848 | bytes 5079584 | tf_op jit(solution)/shard_map/schgp,schpd->schgd/dot_general | solution.py:152
  51.5 0.3 convert_reduce_fusion
  51.8 0.6 copy.141
  52.4 0.6 copy.131
  53.0 4.2 %all-to-all-start.3 = ((f32[4,4,2,4]{3,1,2,0:T(4,128)}), f32[4,4,2,4]{3,1,2,0:T(4,128)S(1)}, u32[]{:S(2)}, u32[]{:S(2)}) async-start(f32[4,4,2,4]{3,1,2,0:T(4,128)} %copy.141), calls=%async_computation.3 | async-start | bytes 32768 | tf_op jit(solution)/shard_map/all_to_all | solution.py:157
  57.5 4.5 %all-to-all-done.3 = f32[4,4,2,4]{3,1,2,0:T(4,128)S(1)} async-done(((f32[4,4,2,4]{3,1,2,0:T(4,128)}), f32[4,4,2,4]{3,1,2,0:T(4,128)S(1)}, u32[]{:S(2)}, u32[]{:S(2)}) %all-to-all-start.3) | async-done | bytes 544 | tf_op jit(solution)/shard_map/all_to_all | solution.py:157
  62.0 3.3 %all-to-all-start.2 = ((f32[4,4,2,4,128]{4,1,3,2,0:T(4,128)}), f32[4,4,2,4,128]{4,1,3,2,0:T(4,128)S(1)}, u32[]{:S(2)}, u32[]{:S(2)}) async-start(f32[4,4,2,4,128]{4,1,3,2,0:T(4,128)} %copy.131), calls=%async_computation.2 | async-start | bytes 131072 | tf_op jit(solution)/shard_map/all_to_all | solution.py:158
  65.6 1.8 all-gather.2
  67.6 1.8 all-gather.1
  70.1 0.2 convolution_bitcast_fusion
  70.4 2.0 fusion.13
  72.4 1.9 all-gather
  74.5 5.2 %fusion.31 = f32[8,4096]{1,0:T(8,128)} fusion(bf16[1024,4096]{1,0:T(8,128)(2,1)} %param.37, bf16[1,8,8,128]{3,2,1,0:T(8,128)(2,1)S(1)} %bitcast.89), kind=kOutput, calls=%fused_computation.61 | convolution fusion | flops 67108864 | bytes 8536064 | tf_op jit(solution)/shard_map/dot_general | solution.py:183
  79.8 0.6 dynamic-slice
  81.1 35.1 %all-reduce.5.cloned.1.call-done = f32[8,4096]{1,0:T(8,128)} async-done(((f32[8,4096]{1,0:T(8,128)}), f32[8,4096]{1,0:T(8,128)}) %all-reduce.5.cloned.1.call-update) | async-done | bytes 131088
  116.2 1.1 multiply_reduce_fusion.1
  117.3 1.0 fusion.35
  118.3 41.7 %all-gather.3 = bf16[16,2,4096]{2,1,0:T(2,128)(2,1)S(1)} all-gather(bf16[1,2,4096]{2,1,0:T(2,128)(2,1)S(1)} %fusion.35), channel_id=1, replica_groups=mesh['group'=4,'depth'=2,'mp'=4] {'group','mp'}, dimensions={0}, use_global_device_ids=true | all-gather | bytes 278528 | tf_op jit(solution)/shard_map/all_gather | solution.py:191
  160.1 4.3 %fusion.63 = f32[32,896]{1,0:T(8,128)S(1)} fusion(bf16[32,4096]{1,0:T(8,128)(2,1)S(1)} %reshape.507, bf16[4096,896]{1,0:T(8,128)(2,1)} %param.39), kind=kOutput, calls=%fused_computation.153 | convolution fusion | flops 234881024 | bytes 7716864 | tf_op jit(solution)/shard_map/dot_general | solution.py:192
  164.4 8.5 %fusion.16 = f32[32,4096]{1,0:T(8,128)} fusion(bf16[896,4096]{1,0:T(8,128)(2,1)} %param.41, bf16[32,4096]{1,0:T(8,128)(2,1)S(1)} %reshape.507, bf16[4096,896]{1,0:T(8,128)(2,1)} %param.40, f32[32,896]{1,0:T(8,128)S(1)} %fusion.63), kind=kOutput, calls=%fused_computation.26 | convolution fusion | flops 469934080 | bytes 15581184 | tf_op jit(solution)/shard_map/dot_general | solution.py:197
  172.9 0.6 dynamic-slice.2
  174.2 104.4 %all-reduce.7.cloned.1.call-done = f32[32,4096]{1,0:T(8,128)} async-done(((f32[32,4096]{1,0:T(8,128)}), f32[32,4096]{1,0:T(8,128)}) %all-reduce.7.cloned.1.call-update) | async-done | bytes 524304
  278.6 1.6 fusion.27
  (101 shorter events, 4.2 us)
Async XLA Ops:
  7.2 24.0 %copy-start = (bf16[8,2,576,128]{3,2,1,0:T(8,128)(2,1)S(1)}, bf16[8,2,576,128]{3,2,1,0:T(8,128)(2,1)}, u32[]{:S(2)}) copy-start(bf16[8,2,576,128]{3,2,1,0:T(8,128)(2,1)} %param.30) | copy-start | bytes 7077892
  7.2 23.2 %copy-start.2 = (bf16[16,8,128]{2,1,0:T(8,128)(2,1)S(1)}, bf16[16,8,128]{2,1,0:T(8,128)(2,1)}, u32[]{:S(2)}) copy-start(bf16[16,8,128]{2,1,0:T(8,128)(2,1)} %param.24) | copy-start | bytes 98308
  7.2 23.2 %copy-start.6 = (bf16[16,2,128]{2,1,0:T(2,128)(2,1)S(1)}, bf16[16,2,128]{2,1,0:T(2,128)(2,1)}, u32[]{:S(2)}) copy-start(bf16[16,2,128]{2,1,0:T(2,128)(2,1)} %param.25) | copy-start | bytes 24580
  16.6 22.8 %all-to-all-start = ((bf16[4,4,8,128]{3,2,1,0:T(8,128)(2,1)}), bf16[4,4,8,128]{3,2,1,0:T(8,128)(2,1)S(1)}, u32[]{:S(2)}, u32[]{:S(2)}) async-start(bf16[4,4,8,128]{3,2,1,0:T(8,128)(2,1)} %broadcast_select_fusion), calls=%async_computation | async-start | bytes 65536 | tf_op jit(solution)/shard_map/all_to_all | solution.py:137
  34.4 5.0 %copy-start.5 = (bf16[16,2,128]{2,1,0:T(2,128)(2,1)S(1)}, bf16[16,2,128]{2,1,0:T(2,128)(2,1)}, u32[]{:S(2)}) copy-start(bf16[16,2,128]{2,1,0:T(2,128)(2,1)} %param.26) | copy-start | bytes 24580
  44.0 9.0 %all-to-all-start.1 = ((f32[4,4,2,4]{3,2,1,0:T(2,128)}), f32[4,4,2,4]{3,2,1,0:T(2,128)S(1)}, u32[]{:S(2)}, u32[]{:S(2)}) async-start(f32[4,4,2,4]{3,2,1,0:T(2,128)} %get-tuple-element.49), calls=%async_computation.1 | async-start | bytes 32768 | tf_op jit(solution)/shard_map/all_to_all | solution.py:156
  53.0 8.9 %all-to-all-start.3 = ((f32[4,4,2,4]{3,1,2,0:T(4,128)}), f32[4,4,2,4]{3,1,2,0:T(4,128)S(1)}, u32[]{:S(2)}, u32[]{:S(2)}) async-start(f32[4,4,2,4]{3,1,2,0:T(4,128)} %copy.141), calls=%async_computation.3 | async-start | bytes 32768 | tf_op jit(solution)/shard_map/all_to_all | solution.py:157
  62.0 8.2 %all-to-all-start.2 = ((f32[4,4,2,4,128]{4,1,3,2,0:T(4,128)}), f32[4,4,2,4,128]{4,1,3,2,0:T(4,128)S(1)}, u32[]{:S(2)}, u32[]{:S(2)}) async-start(f32[4,4,2,4,128]{4,1,3,2,0:T(4,128)} %copy.131), calls=%async_computation.2 | async-start | bytes 131072 | tf_op jit(solution)/shard_map/all_to_all | solution.py:158
  65.2 51.0 %all-reduce.5.cloned.1.call-start = ((), (), s32[]{:S(2)}) async-start(), calls=%async_computation.4 | async-start | bytes 262144
  74.4 5.3 %copy-start.3 = (bf16[8,8,128]{2,1,0:T(8,128)(2,1)}, bf16[8,8,128]{2,1,0:T(8,128)(2,1)S(1)}, u32[]{:S(2)}) copy-start(bf16[8,8,128]{2,1,0:T(8,128)(2,1)S(1)} %fusion.28) | copy-start | bytes 49156
  74.5 5.3 %copy-start.8 = (u32[32]{0:T(128)S(1)}, u32[32]{0:T(128)}, u32[]{:S(2)}) copy-start(u32[32]{0:T(128)} %constant.204) | copy-start | bytes 388
  74.5 41.7 %copy-start.1 = (bf16[2,4096]{1,0:T(2,128)(2,1)S(1)}, bf16[2,4096]{1,0:T(2,128)(2,1)}, u32[]{:S(2)}) copy-start(bf16[2,4096]{1,0:T(2,128)(2,1)} %param.23) | copy-start | bytes 49156
  74.5 42.8 %copy-start.4 = (f32[4096]{0:T(1024)S(1)}, f32[4096]{0:T(1024)}, u32[]{:S(2)}) copy-start(f32[4096]{0:T(1024)} %param.38) | copy-start | bytes 49156
  79.8 198.8 %all-reduce.7.cloned.1.call-start = ((), (), s32[]{:S(2)}) async-start(), calls=%async_computation.5 | async-start | bytes 1048576
  164.4 8.6 %copy-start.7 = (u32[32]{0:T(128)S(1)}, u32[32]{0:T(128)}, u32[]{:S(2)}) copy-start(u32[32]{0:T(128)} %constant.208) | copy-start | bytes 388
Sparse Core Ops, SparseCore 0:
  79.9 36.2 all-reduce.4
  173.0 105.4 all-reduce.6
where the time goes:
time: 288 us; the launch traced here: 287 us
  waiting for transfers between devices  144 us (50%)
  blocking collectives  47.2 us (16%)
  matrix products  30.2 us (10%)
  local copies, waits for them, and re-layouts  21.6 us (8%)
  starting transfers between devices  16.9 us (6%)
  between operations  15.7 us (5%)
  other arithmetic  11.2 us (4%)
    unnamed x4, waiting for transfers between devices  140 us
    all_gather x1, blocking collectives, on_device(): piece = lax.all_gather(normed, ('group', 'mp'), axis=0, tiled=True)  41.7 us
    dot_general x1, matrix products, on_device(): jnp.dot(picked_rows, down_weight, preferred_element_type=jnp.float32)  8.51 us
  transfers between devices with their start and end apart: 6, of which 3 were waited for; matrix products, arithmetic and copies ran while one was open for 9% of the time, Pallas kernels for 0%

commit v1 on v0

--- a/solution.py
+++ b/solution.py
@@ -188,7 +188,15 @@
     residual = states.astype(jnp.float32) + projected
     spread = jnp.mean(residual * residual, axis=-1, keepdims=True)
     normed = (residual * lax.rsqrt(spread + NORM_EPSILON) * norm_gain).astype(jnp.bfloat16)
-    piece = lax.all_gather(normed, ("group", "mp"), axis=0, tiled=True)
+    piece = jnp.concatenate(
+        jax.lax.all_to_all(
+            jnp.stack([normed for _ in range(jax.lax.psum(1, ("group", "mp")))], 0),
+            ("group", "mp"),
+            0,
+            0,
+        ),
+        0,
+    )
     gate_term = jnp.dot(piece, gate_weight, preferred_element_type=jnp.float32)
     up_term = jnp.dot(piece, up_weight, preferred_element_type=jnp.float32)
     hidden = (jax.nn.silu(gate_term) * up_term).astype(jnp.bfloat16)

time: 288 us -> 262 us (0.910)
  blocking collectives: 47.2 us -> 19.5 us
    all_gather x1 -> x0, blocking collectives: 41.7 us -> none  [on_device(): piece = lax.all_gather(normed, ('group', 'mp'), axis=0, tiled=True)]
    all_to_all x0 -> x1, blocking collectives: none -> 13.9 us  [on_device(): jax.lax.all_to_all(jnp.stack([normed for _ in range(jax.lax.psum(1, ('gro...]
  transfers between devices with their start and end apart: 6 -> 6, of which waited for: 3 -> 3; matrix products, arithmetic and copies ran while one was open for 9% -> 10% of each run, Pallas kernels for 0% -> 0%
where the time goes in v1:
time: 262 us; the launch traced here: 261 us
  waiting for transfers between devices  145 us (55%)
  matrix products  30.2 us (12%)
  local copies, waits for them, and re-layouts  21.8 us (8%)
  blocking collectives  19.5 us (7%)
  starting transfers between devices  16.9 us (6%)
  between operations  15.7 us (6%)
  other arithmetic  11.2 us (4%)
    unnamed x4, waiting for transfers between devices  141 us
    all_to_all x1, blocking collectives, on_device(): jax.lax.all_to_all(jnp.stack([normed for _ in range(jax.lax.psum(1, ('gro...  13.9 us
    dot_general x1, matrix products, on_device(): jnp.dot(picked_rows, down_weight, preferred_element_type=jnp.float32)  8.51 us
    all_gather x3, blocking collectives, merged(): gathered = jax.tree.map(lambda a: lax.all_gather(a, axis), part)  5.54 us
  transfers between devices with their start and end apart: 6, of which 3 were waited for; matrix products, arithmetic and copies ran while one was open for 10% of the time, Pallas kernels for 0%

profile of v1, /device:TPU:0, one launch (start us, length us, event | category | flops | bytes accessed | tf_op | source)
XLA Modules:
  0.0 260.5 jit_solution(16473309175646977907)
XLA Ops:
  7.2 0.8 fusion.51
  8.1 0.7 gather_fusion.3
  8.8 1.3 gather_fusion.4
  10.1 1.2 dynamic_slice.43
  11.4 0.7 broadcast_compare_fusion.3
  12.4 0.2 multiply_reduce_fusion.2
  12.8 0.7 add.205
  13.5 0.9 select_reduce_fusion.4
  14.6 1.3 gather_fusion.2
  15.9 0.7 broadcast_select_fusion
  16.6 5.2 %all-to-all-start = ((bf16[4,4,8,128]{3,2,1,0:T(8,128)(2,1)}), bf16[4,4,8,128]{3,2,1,0:T(8,128)(2,1)S(1)}, u32[]{:S(2)}, u32[]{:S(2)}) async-start(bf16[4,4,8,128]{3,2,1,0:T(8,128)(2,1)} %broadcast_select_fusion), calls=%async_computation | async-start | bytes 65536 | tf_op jit(solution)/shard_map/all_to_all | solution.py:137
  21.8 0.8 copy.120
  22.6 0.7 broadcast_compare_fusion.1
  23.3 0.6 gather_fusion
  24.1 1.4 gather_fusion.1
  26.1 0.2 select_reduce_fusion.3
  26.4 0.6 multiply_reduce_fusion
  27.2 0.7 broadcast_compare_fusion
  27.9 2.3 select_reduce_fusion.1
  30.8 0.2 convert_reduce_fusion.1
  31.1 3.3 %gather_fusion.5 = bf16[16,2,576,128]{3,2,1,0:T(8,128)(2,1)} fusion(bf16[8,2,576,128]{3,2,1,0:T(8,128)(2,1)S(1)} %copy-done, s32[1024]{0:T(1024)S(1)} %pad_clamp_fusion), kind=kCustom, calls=%fused_computation.1.clone | custom fusion | bytes 9437248 | tf_op jit(solution)/shard_map/jit(_take)/gather | solution.py:139
  34.5 5.0 %gather_fusion.6 = bf16[16,2,576,128]{3,2,1,0:T(8,128)(2,1)} fusion(bf16[8,2,576,128]{3,2,1,0:T(8,128)(2,1)} %param.31, s32[1024]{0:T(1024)S(1)} %pad_clamp_fusion), kind=kCustom, calls=%fused_computation.3.clone | custom fusion | bytes 9437248 | tf_op jit(solution)/shard_map/jit(_take)/gather | solution.py:140
  39.4 4.0 %select_reduce_fusion = (f32[4,4,2,4]{3,2,1,0:T(2,128)S(1)}, f32[4,4,2,4,576]{4,3,2,1,0:T(4,128)S(1)}) fusion(pred[4,4]{1,0:T(4,128)(4,1)S(1)} %bitcast.96, bf16[4,4,2,4,128]{4,3,2,1,0:T(4,128)(2,1)S(1)} %bitcast.89, bf16[4,4,2,576,128]{4,3,2,1,0:T(8,128)(2,1)} %bitcast.81, pred[4,4]{1,0:T(4,128)(4,1)S(1)} %compare_and_fusion.1), kind=kOutput, calls=%fused_computation.29 | convolution fusion | flops 21454720 | bytes 5046816 | tf_op jit(solution)/shard_map/schgd,schpd->schgp/dot_general | solution.py:142
  43.4 0.6 multiply_floor_fusion
  44.0 4.2 %all-to-all-start.1 = ((f32[4,4,2,4]{3,2,1,0:T(2,128)}), f32[4,4,2,4]{3,2,1,0:T(2,128)S(1)}, u32[]{:S(2)}, u32[]{:S(2)}) async-start(f32[4,4,2,4]{3,2,1,0:T(2,128)} %get-tuple-element.49), calls=%async_computation.1 | async-start | bytes 32768 | tf_op jit(solution)/shard_map/all_to_all | solution.py:156
  48.2 3.2 %fusion = f32[4,4,2,4,128]{4,3,2,1,0:T(4,128)S(1)} fusion(bf16[4,4,2,576,128]{4,3,2,1,0:T(8,128)(2,1)} %bitcast.80, pred[4,4]{1,0:T(4,128)(4,1)S(1)} %compare_and_fusion.1, f32[4,4,2,4,576]{4,3,2,1,0:T(4,128)S(1)} %get-tuple-element.53, f32[4,4,2,4]{3,2,1,0:T(2,128)S(1)} %get-tuple-element.50, pred[4,4]{1,0:T(4,128)(4,1)S(1)} %bitcast.97), kind=kOutput, calls=%fused_computation.7 | convolution fusion | flops 21454848 | bytes 5079584 | tf_op jit(solution)/shard_map/schgp,schpd->schgd/dot_general | solution.py:152
  51.5 0.3 convert_reduce_fusion
  51.8 0.6 copy.141
  52.4 0.6 copy.131
  53.0 4.2 %all-to-all-start.3 = ((f32[4,4,2,4]{3,1,2,0:T(4,128)}), f32[4,4,2,4]{3,1,2,0:T(4,128)S(1)}, u32[]{:S(2)}, u32[]{:S(2)}) async-start(f32[4,4,2,4]{3,1,2,0:T(4,128)} %copy.141), calls=%async_computation.3 | async-start | bytes 32768 | tf_op jit(solution)/shard_map/all_to_all | solution.py:157
  57.5 4.5 %all-to-all-done.3 = f32[4,4,2,4]{3,1,2,0:T(4,128)S(1)} async-done(((f32[4,4,2,4]{3,1,2,0:T(4,128)}), f32[4,4,2,4]{3,1,2,0:T(4,128)S(1)}, u32[]{:S(2)}, u32[]{:S(2)}) %all-to-all-start.3) | async-done | bytes 544 | tf_op jit(solution)/shard_map/all_to_all | solution.py:157
  62.0 3.3 %all-to-all-start.2 = ((f32[4,4,2,4,128]{4,1,3,2,0:T(4,128)}), f32[4,4,2,4,128]{4,1,3,2,0:T(4,128)S(1)}, u32[]{:S(2)}, u32[]{:S(2)}) async-start(f32[4,4,2,4,128]{4,1,3,2,0:T(4,128)} %copy.131), calls=%async_computation.2 | async-start | bytes 131072 | tf_op jit(solution)/shard_map/all_to_all | solution.py:158
  65.6 1.8 all-gather.2
  67.6 1.8 all-gather.1
  70.1 0.2 convolution_bitcast_fusion
  70.4 2.0 fusion.13
  72.4 1.9 all-gather
  74.5 5.2 %fusion.31 = f32[8,4096]{1,0:T(8,128)} fusion(bf16[1024,4096]{1,0:T(8,128)(2,1)} %param.37, bf16[1,8,8,128]{3,2,1,0:T(8,128)(2,1)S(1)} %bitcast.87), kind=kOutput, calls=%fused_computation.61 | convolution fusion | flops 67108864 | bytes 8536064 | tf_op jit(solution)/shard_map/dot_general | solution.py:183
  79.8 0.6 dynamic-slice
  81.1 35.1 %all-reduce.5.cloned.1.call-done = f32[8,4096]{1,0:T(8,128)} async-done(((f32[8,4096]{1,0:T(8,128)}), f32[8,4096]{1,0:T(8,128)}) %all-reduce.5.cloned.1.call-update) | async-done | bytes 131088
  116.2 1.1 multiply_reduce_fusion.1
  117.3 1.0 multiply_convert_fusion
  118.5 13.9 %all_to_all.25 = bf16[16,2,4096]{2,1,0:T(2,128)(2,1)S(1)} all-to-all(bf16[16,2,4096]{2,1,0:T(2,128)(2,1)S(1)} %stack.2), channel_id=1, replica_groups=mesh['group'=4,'depth'=2,'mp'=4] {'group','mp'}, dimensions={0} | all-to-all | bytes 524288 | tf_op jit(solution)/shard_map/all_to_all | solution.py:192
  132.5 4.3 %fusion.62 = f32[32,896]{1,0:T(8,128)S(1)} fusion(bf16[32,4096]{1,0:T(8,128)(2,1)S(1)} %reshape.433, bf16[4096,896]{1,0:T(8,128)(2,1)} %param.39), kind=kOutput, calls=%fused_computation.152 | convolution fusion | flops 234881024 | bytes 7716864 | tf_op jit(solution)/shard_map/dot_general | solution.py:200
  136.8 8.5 %fusion.16 = f32[32,4096]{1,0:T(8,128)} fusion(bf16[896,4096]{1,0:T(8,128)(2,1)} %param.41, bf16[32,4096]{1,0:T(8,128)(2,1)S(1)} %reshape.433, bf16[4096,896]{1,0:T(8,128)(2,1)} %param.40, f32[32,896]{1,0:T(8,128)S(1)} %fusion.62), kind=kOutput, calls=%fused_computation.26 | convolution fusion | flops 469934080 | bytes 15581184 | tf_op jit(solution)/shard_map/dot_general | solution.py:205
  145.3 0.6 dynamic-slice.2
  146.6 105.5 %all-reduce.7.cloned.1.call-done = f32[32,4096]{1,0:T(8,128)} async-done(((f32[32,4096]{1,0:T(8,128)}), f32[32,4096]{1,0:T(8,128)}) %all-reduce.7.cloned.1.call-update) | async-done | bytes 524304
  252.1 1.6 fusion.27
  (102 shorter events, 4.4 us)
Async XLA Ops:
  7.2 24.0 %copy-start = (bf16[8,2,576,128]{3,2,1,0:T(8,128)(2,1)S(1)}, bf16[8,2,576,128]{3,2,1,0:T(8,128)(2,1)}, u32[]{:S(2)}) copy-start(bf16[8,2,576,128]{3,2,1,0:T(8,128)(2,1)} %param.30) | copy-start | bytes 7077892
  7.2 23.2 %copy-start.2 = (bf16[16,8,128]{2,1,0:T(8,128)(2,1)S(1)}, bf16[16,8,128]{2,1,0:T(8,128)(2,1)}, u32[]{:S(2)}) copy-start(bf16[16,8,128]{2,1,0:T(8,128)(2,1)} %param.24) | copy-start | bytes 98308
  7.2 23.2 %copy-start.6 = (bf16[16,2,128]{2,1,0:T(2,128)(2,1)S(1)}, bf16[16,2,128]{2,1,0:T(2,128)(2,1)}, u32[]{:S(2)}) copy-start(bf16[16,2,128]{2,1,0:T(2,128)(2,1)} %param.25) | copy-start | bytes 24580
  16.6 22.8 %all-to-all-start = ((bf16[4,4,8,128]{3,2,1,0:T(8,128)(2,1)}), bf16[4,4,8,128]{3,2,1,0:T(8,128)(2,1)S(1)}, u32[]{:S(2)}, u32[]{:S(2)}) async-start(bf16[4,4,8,128]{3,2,1,0:T(8,128)(2,1)} %broadcast_select_fusion), calls=%async_computation | async-start | bytes 65536 | tf_op jit(solution)/shard_map/all_to_all | solution.py:137
  34.4 5.0 %copy-start.5 = (bf16[16,2,128]{2,1,0:T(2,128)(2,1)S(1)}, bf16[16,2,128]{2,1,0:T(2,128)(2,1)}, u32[]{:S(2)}) copy-start(bf16[16,2,128]{2,1,0:T(2,128)(2,1)} %param.26) | copy-start | bytes 24580
  44.0 9.0 %all-to-all-start.1 = ((f32[4,4,2,4]{3,2,1,0:T(2,128)}), f32[4,4,2,4]{3,2,1,0:T(2,128)S(1)}, u32[]{:S(2)}, u32[]{:S(2)}) async-start(f32[4,4,2,4]{3,2,1,0:T(2,128)} %get-tuple-element.49), calls=%async_computation.1 | async-start | bytes 32768 | tf_op jit(solution)/shard_map/all_to_all | solution.py:156
  53.0 8.9 %all-to-all-start.3 = ((f32[4,4,2,4]{3,1,2,0:T(4,128)}), f32[4,4,2,4]{3,1,2,0:T(4,128)S(1)}, u32[]{:S(2)}, u32[]{:S(2)}) async-start(f32[4,4,2,4]{3,1,2,0:T(4,128)} %copy.141), calls=%async_computation.3 | async-start | bytes 32768 | tf_op jit(solution)/shard_map/all_to_all | solution.py:157
  62.0 8.2 %all-to-all-start.2 = ((f32[4,4,2,4,128]{4,1,3,2,0:T(4,128)}), f32[4,4,2,4,128]{4,1,3,2,0:T(4,128)S(1)}, u32[]{:S(2)}, u32[]{:S(2)}) async-start(f32[4,4,2,4,128]{4,1,3,2,0:T(4,128)} %copy.131), calls=%async_computation.2 | async-start | bytes 131072 | tf_op jit(solution)/shard_map/all_to_all | solution.py:158
  65.2 51.0 %all-reduce.5.cloned.1.call-start = ((), (), s32[]{:S(2)}) async-start(), calls=%async_computation.5 | async-start | bytes 262144
  74.4 5.3 %copy-start.3 = (bf16[8,8,128]{2,1,0:T(8,128)(2,1)}, bf16[8,8,128]{2,1,0:T(8,128)(2,1)S(1)}, u32[]{:S(2)}) copy-start(bf16[8,8,128]{2,1,0:T(8,128)(2,1)S(1)} %fusion.28) | copy-start | bytes 49156
  74.5 5.3 %copy-start.8 = (u32[32]{0:T(128)S(1)}, u32[32]{0:T(128)}, u32[]{:S(2)}) copy-start(u32[32]{0:T(128)} %constant.204) | copy-start | bytes 388
  74.5 41.7 %copy-start.1 = (bf16[2,4096]{1,0:T(2,128)(2,1)S(1)}, bf16[2,4096]{1,0:T(2,128)(2,1)}, u32[]{:S(2)}) copy-start(bf16[2,4096]{1,0:T(2,128)(2,1)} %param.23) | copy-start | bytes 49156
  74.5 42.8 %copy-start.4 = (f32[4096]{0:T(1024)S(1)}, f32[4096]{0:T(1024)}, u32[]{:S(2)}) copy-start(f32[4096]{0:T(1024)} %param.38) | copy-start | bytes 49156
  79.8 172.3 %all-reduce.7.cloned.1.call-start = ((), (), s32[]{:S(2)}) async-start(), calls=%async_computation.6 | async-start | bytes 1048576
  136.8 8.6 %copy-start.7 = (u32[32]{0:T(128)S(1)}, u32[32]{0:T(128)}, u32[]{:S(2)}) copy-start(u32[32]{0:T(128)} %constant.208) | copy-start | bytes 388
Sparse Core Ops, SparseCore 0:
  79.9 36.2 all-reduce.4
  145.5 106.5 all-reduce.6
